TPU v7x, 128 devices: a whole 4x4x4 slice. The times are simulated.
128 devices in a mesh: row: 16 (over y_lo, z, core), col: 8 (over y_hi, x).
Axes of the slice: x: 4, y: 4 (y_hi: 2, y_lo: 2; y = y_hi * 2 + y_lo), z: 4, core: 2. Of those that a mesh axis runs over, the one named last changes fastest.
Arguments:
- matrix: float32 [3456, 131072], P('row', 'col'), may hold values from -6 to 6
- range_basis: float32 [3456, 384], P('col', 'row'), may hold values from -0.125 to 0.125
Outputs:
- projected: float32 [384, 131072], P('row')
All inputs are finite; a program needn't handle non-finite values.
Results may differ from a plain program's by a relative error of at most 0.000071.
Values sent between devices are 32-bit elements; how exact they have to be, the bound alone decides.
A program may use at most 128 MiB of HBM per device.

v0:
```python
import jax
import jax.numpy as jnp
from jax import lax
from jax.sharding import PartitionSpec as P


def copy_for_each(shard, axis):
    length = lax.axis_size(axis)
    return lax.all_to_all(
        jnp.broadcast_to(shard[None], (length, *shard.shape)), axis, 0, 0, tiled=True
    )


def joined_along(parts, dim):
    lengths = list(parts.shape[1:])
    lengths[dim] *= parts.shape[0]
    return jnp.moveaxis(parts, 0, dim).reshape(lengths)


def gathered_copies(shard, axis, dim):
    parts = copy_for_each(shard, axis)
    return joined_along(parts, dim)


def project(left, right):
    return lax.dot_general(
        left,
        right,
        (((0,), (0,)), ((), ())),
        precision=lax.Precision.HIGHEST,
        preferred_element_type=jnp.float32,
    )


def per_device(matrix, range_basis):
    row_panel = gathered_copies(range_basis, "col", 0)
    local_basis = lax.all_to_all(row_panel, "row", split_axis=0, concat_axis=1, tiled=True)
    owned_rows = lax.psum_scatter(
        project(local_basis, matrix), "row", scatter_dimension=0, tiled=True
    )
    return lax.all_gather(owned_rows, "col", axis=1, tiled=True)


def solution(mesh):
    in_specs = (P("row", "col"), P("col", "row"))
    out_specs = P("row", None)
    return jax.shard_map(
        per_device, mesh=mesh, in_specs=in_specs, out_specs=out_specs, check_vma=False
    )
```

profile of v0, /device:TPU:0, one launch (start us, length us, event | category | flops | bytes accessed | tf_op | source)
XLA Modules:
  0.0 366.7 jit_solution(5536820550529386363)
XLA Ops:
  6.5 0.0 reduce-scatter.2.cloned.1.call-start
  6.5 0.8 broadcast_in_dim.2
  7.4 17.0 %all_to_all.24 = f32[8,432,24]{1,2,0:T(8,128)S(1)} all-to-all(f32[8,432,24]{1,2,0:T(8,128)S(1)} %broadcast_in_dim.2), channel_id=1, replica_groups=mesh['row'=16,'col'=8] {'col'}, dimensions={0} | all-to-all | bytes 663552 | tf_op jit(solution)/shard_map/all_to_all | solution.py:9
  24.4 0.2 copy.6
  24.6 0.1 all_to_all.18
  24.8 0.2 copy.7
  25.0 14.8 %all_to_all.25 = f32[16,216,24]{1,2,0:T(8,128)S(1)} all-to-all(f32[16,216,24]{1,2,0:T(8,128)S(1)} %copy.7), channel_id=1, replica_groups=mesh['row'=16,'col'=8] {'row'}, dimensions={0} | all-to-all | bytes 663552 | tf_op jit(solution)/shard_map/all_to_all | solution.py:37
  39.7 25.4 %fusion = f32[384,16384]{1,0:T(8,128)} fusion(f32[216,384]{0,1:T(8,128)S(1)} %bitcast.7, f32[216,16384]{1,0:T(8,128)} %param.2), kind=kOutput, calls=%fused_computation | convolution fusion | flops 16307453952 | bytes 39653376 | tf_op jit(solution)/shard_map/dot_general | solution.py:26
  65.1 0.0 reduce-scatter.2.cloned.1.call-update
  65.2 0.0 all-gather.2.cloned.1.call-start
  65.2 136.7 %reduce-scatter.2.cloned.1.call-done = f32[24,16384]{1,0:T(8,128)} async-done(((f32[384,16384]{1,0:T(8,128)}), f32[24,16384]{1,0:T(8,128)}) %reduce-scatter.2.cloned.1.call-update) | async-done | bytes 1572880 | tf_op jit(solution)/shard_map/reduce_scatter | solution.py:38
  202.0 0.0 all-gather.2.cloned.1.call-update
  202.0 147.7 %all-gather.2.cloned.1.call-done = f32[24,131072]{1,0:T(8,128)} async-done(((f32[24,16384]{1,0:T(8,128)}), f32[24,131072]{1,0:T(8,128)}) %all-gather.2.cloned.1.call-update) | async-done | bytes 12582928 | tf_op jit(solution)/shard_map/all_gather | solution.py:41
  349.7 10.2 %copy.9 = f32[24,131072]{1,0:T(8,128)} copy(f32[24,131072]{1,0:T(8,128)} %all-gather.2.cloned.1.call-done) | data formatting | bytes 25165824
Async XLA Ops:
  6.5 195.4 %reduce-scatter.2.cloned.1.call-start = ((), (), s32[]{:S(2)}) async-start(), calls=%async_computation.3 | async-start | bytes 26738688 | tf_op jit(solution)/shard_map/reduce_scatter | solution.py:38
  65.2 284.5 %all-gather.2.cloned.1.call-start = ((), (), s32[]{:S(2)}) async-start(), calls=%async_computation.4 | async-start | bytes 14155776 | tf_op jit(solution)/shard_map/all_gather | solution.py:41
Sparse Core Ops, SparseCore 0:
  65.3 136.6 reduce-scatter.1
  204.3 145.3 all-gather.1
where the time goes:
time: 367 us
  waiting for transfers between devices  285 us (78%)
  blocking collectives  31.8 us (9%)
  matrix products  25.4 us (7%)
  between operations  13.4 us (4%)
  local copies, waits for them, and re-layouts  11.6 us (3%)
    all_gather x1, waiting for transfers between devices, per_device(): return lax.all_gather(owned_rows, 'col', axis=1, tiled=True)  148 us
    reduce_scatter x1, waiting for transfers between devices, per_device(): lax.psum_scatter(project(local_basis, matrix), 'row', scatter_dimension=0...  137 us
    dot_general x1, matrix products, project(): lax.dot_general(left, right, (((0,), (0,)), ((), ())), precision=lax.Prec...  25.4 us
    all_to_all x1, blocking collectives, copy_for_each(): lax.all_to_all(jnp.broadcast_to(shard[None], (length, *shard.shape)), axi...  17 us
    all_to_all x1, blocking collectives, per_device(): lax.all_to_all(row_panel, 'row', split_axis=0, concat_axis=1, tiled=True)  14.8 us
    unnamed x1, local copies, waits for them, and re-layouts  10.2 us
  transfers between devices with their start and end apart: 2, of which 2 were waited for; matrix products, arithmetic and copies ran while one was open for 0% of the time, Pallas kernels for 0%

commit v1 on v0

v1 whole, which is shorter than its diff:
```python
import functools

import jax
import jax.numpy as jnp
from jax import lax
from jax.experimental import pallas as pl
from jax.experimental.pallas import tpu as pltpu
from jax.sharding import PartitionSpec as P

MESH = pl.DeviceIdType.MESH
STEPS = 16
SLOTS = 8
F32 = jnp.float32
BF16 = jnp.bfloat16


def halves(value):
    high = value.astype(BF16)
    return high, (value - high.astype(F32)).astype(BF16)


def dot(left, right):
    return jnp.dot(left, right, preferred_element_type=F32)


def kernel(
    steps, a_ref, q_ref, o_ref,
    ab, qf, qhi, qlo, p, zr, yr, out,
    a_own, a_send, a_recv, q_send, q_recv, f_send, f_recv,
    z_send, z_recv, y_send, y_recv, c_send, c_recv, h_send, h_recv, x_send, x_recv, o_sem,
):
    rows, width = a_ref.shape
    basis = q_ref.shape[0]
    piece = width // steps
    half = piece // 2
    w = half // 2

    r, c = lax.axis_index("row"), lax.axis_index("col")
    k = lax.rem(r, 2)
    j = lax.div(r, 2)
    z = lax.rem(j, 4)
    ylo = lax.div(j, 4)
    x = lax.rem(c, 4)
    yhi = lax.div(c, 4)

    def row_of(ylo_, z_, k_):
        return (ylo_ * 4 + z_) * 2 + k_

    def wrap(v):
        return lax.rem(v + 8, 4)

    sibling = (row_of(ylo, z, 1 - k), c)
    z_next = [(row_of(ylo, wrap(z + 1), k), c), (row_of(ylo, wrap(z - 1), k), c)]
    y_pair = (row_of(1 - ylo, z, k), c)
    h_pair = (r, (1 - yhi) * 4 + x)
    x_next = [(r, yhi * 4 + wrap(x + 1)), (r, yhi * 4 + wrap(x - 1))]

    def remote(src, dst, send, recv, device):
        return pltpu.make_async_remote_copy(
            src_ref=src, dst_ref=dst, send_sem=send, recv_sem=recv,
            device_id=device, device_id_type=MESH,
        )

    def a_local(s):
        cols = pl.ds(pl.multiple_of(s * piece + k * half, 128), half)
        at = pl.ds(pl.multiple_of(k * rows, 8), rows)
        return pltpu.make_async_copy(a_ref.at[:, cols], ab.at[s, at], a_own.at[s])

    def a_swap(s):
        cols = pl.ds(pl.multiple_of(s * piece + (1 - k) * half, 128), half)
        at = pl.ds(pl.multiple_of(k * rows, 8), rows)
        return remote(a_ref.at[:, cols], ab.at[s, at], a_send.at[s], a_recv.at[s], sibling)

    def q_rows(q, k_):
        at = lax.rem(q, 4) * (4 * basis) + lax.div(q, 4) * (2 * basis) + k_ * basis
        return pl.ds(pl.multiple_of(at, 8), basis)

    def q_push(t):
        return remote(q_ref, qf.at[q_rows(j, k)], q_send.at[t], q_recv.at[j], (c * 2 + k, t))

    def q_here():
        return pltpu.make_async_copy(q_ref, qf.at[q_rows(j, k)], q_recv.at[j])

    def q_landed(q):
        return remote(q_ref, qf.at[q_rows(q, k)], q_send.at[q], q_recv.at[q], sibling)

    def q_forward(q):
        block = qf.at[q_rows(q, k)]
        return remote(block, block, f_send.at[q], f_recv.at[q], sibling)

    def z_rows(t, d):
        at = wrap(z - (1 - 2 * d) * (t + 1)) * (4 * basis)
        return pl.ds(pl.multiple_of(at, 8), 4 * basis)

    def z_copy(t, d, s):
        slot = lax.rem(s, SLOTS)
        u = s * 2 + d
        return remote(
            p.at[u, z_rows(t, d)], zr.at[t, u], z_send.at[t, d, slot], z_recv.at[t, d, slot], z_next[d]
        )

    def mine(ylo_, size, first):
        at = z * (4 * basis) + ylo_ * (2 * basis) + first * basis
        return pl.ds(pl.multiple_of(at, 8), size * basis)

    def y_copy(d, s):
        slot = lax.rem(s, SLOTS)
        u = s * 2 + d
        return remote(
            p.at[u, mine(1 - ylo, 2, 0)], yr.at[u], y_send.at[d, slot], y_recv.at[d, slot], y_pair
        )

    def part_cols(k_, d, s):
        at = c * width + s * piece + k_ * half + d * w
        return pl.ds(pl.multiple_of(at, 128), w)

    def c_copy(d, s):
        slot = lax.rem(s, SLOTS)
        return remote(
            p.at[s * 2 + d, mine(ylo, 1, 1 - k)], out.at[:, part_cols(k, d, s)],
            c_send.at[d, slot], c_recv.at[d, slot], sibling,
        )

    def cols_of(yhi_, x_, s):
        at = (yhi_ * 4 + x_) * width + s * piece
        return pl.ds(pl.multiple_of(at, 128), piece)

    def h_copy(s):
        slot = lax.rem(s, SLOTS)
        block = out.at[:, cols_of(yhi, x, s)]
        return remote(block, block, h_send.at[slot], h_recv.at[slot], h_pair)

    x_plan = [
        (yhi, x, 0), (yhi, x, 1), (yhi, wrap(x - 1), 0),
        (1 - yhi, x, 0), (1 - yhi, x, 1), (1 - yhi, wrap(x + 1), 1),
    ]

    def x_copy(m, s):
        slot = lax.rem(s, SLOTS)
        yhi_, x_, d = x_plan[m]
        block = out.at[:, cols_of(yhi_, x_, s)]
        return remote(block, block, x_send.at[m, slot], x_recv.at[m, slot], x_next[d])

    def flush(s, t):
        block = pl.ds(pl.multiple_of(t * width + s * piece, 128), piece)
        return pltpu.make_async_copy(out.at[:, block], o_ref.at[:, block], o_sem.at[t, lax.rem(s, SLOTS)])

    @pl.loop(0, steps)
    def _(s):
        a_local(s).start()

    at_home = c == j
    barrier = pltpu.get_barrier_semaphore()
    for device in [sibling, *z_next, y_pair, h_pair, *x_next]:
        pl.semaphore_signal(barrier, inc=1, device_id=device, device_id_type=MESH)

    @pl.loop(0, 8)
    def _(q):
        @pl.when(jnp.logical_not(jnp.logical_and(at_home, q == j)))
        def _():
            pl.semaphore_signal(barrier, inc=1, device_id=(2 * q + k, j), device_id_type=MESH)

    pl.semaphore_wait(barrier, 15 - jnp.where(at_home, 1, 0))

    @pl.loop(0, 8)
    def _(t):
        home = jnp.logical_and(at_home, t == c)

        @pl.when(jnp.logical_not(home))
        def _():
            q_push(t).start()

        @pl.when(home)
        def _():
            q_here().start()

    @pl.loop(0, steps)
    def _(s):
        a_swap(s).start()

    @pl.loop(0, 8)
    def _(q):
        q_landed(q).wait_recv()
        q_forward(q).start()

    @pl.loop(0, 8)
    def _(q):
        q_forward(q).wait_recv()

    high, low = halves(qf[...])
    qhi[...] = high
    qlo[...] = low

    def compute(s):
        a_local(s).wait()
        a_swap(s).wait_recv()
        for d in range(2):
            a_high, a_low = halves(ab[s, :, d * w : (d + 1) * w])
            p[s * 2 + d] = dot(qhi[...], a_low) + dot(qlo[...], a_high) + dot(qhi[...], a_high)
        for d in range(2):
            z_copy(0, d, s).start()

    def z_add(t, d, s):
        z_copy(t - 1, d, s).wait_recv()
        u = s * 2 + d
        at = z_rows(t, d)
        p[u, at] = p[u, at] + zr[t - 1, u]

    def live(i, lag, body):
        @pl.when(jnp.logical_and(i >= lag, i < steps + lag))
        def _():
            body(i - lag)

    def z_last(s):
        for d in range(2):
            z_add(3, d, s)
            y_copy(d, s).start()

    def z_step(t):
        def body(s):
            for d in range(2):
                z_add(t, d, s)
                z_copy(t, d, s).start()
        return body

    def y_last(s):
        for d in range(2):
            y_copy(d, s).wait_recv()
            u = s * 2 + d
            own, other = mine(ylo, 1, k), mine(ylo, 1, 1 - k)
            y_own = pl.ds(pl.multiple_of(k * basis, 8), basis)
            y_other = pl.ds(pl.multiple_of((1 - k) * basis, 8), basis)
            p[u, other] = p[u, other] + yr[u, y_other]
            c_copy(d, s).start()
            out[:, part_cols(k, d, s)] = p[u, own] + yr[u, y_own]

    def spread(s):
        for d in range(2):
            c_copy(d, s).wait_recv()
        h_copy(s).start()
        x_copy(0, s).start()
        x_copy(1, s).start()

    def spread_far(s):
        h_copy(s).wait_recv()
        x_copy(3, s).start()
        x_copy(4, s).start()

    def forward(m, first):
        def body(s):
            x_copy(first, s).wait_recv()
            x_copy(m, s).start()
        return body

    def retire(s):
        for d in range(2):
            for t in range(3):
                z_copy(t, d, s).wait_send()
            y_copy(d, s).wait_send()
            c_copy(d, s).wait_send()
        h_copy(s).wait_send()
        for m in (1, 2, 3, 5):
            x_copy(m, s).wait_recv()
        for m in range(6):
            x_copy(m, s).wait_send()

        @pl.when(s >= SLOTS)
        def _():
            @pl.loop(0, 8)
            def _(t):
                flush(s - SLOTS, t).wait()

        @pl.loop(0, 8)
        def _(t):
            flush(s, t).start()

    compute(0)

    @pl.loop(0, steps + 6)
    def _(i):
        live(i, 3, z_last)
        live(i, 2, z_step(2))
        live(i, 1, z_step(1))

        @pl.when(i + 1 < steps)
        def _():
            compute(i + 1)

        live(i, 3, y_last)
        live(i, 4, spread_far)
        live(i, 4, forward(2, 0))
        live(i, 5, forward(5, 4))
        live(i, 3, spread)
        live(i, 6, retire)

    @pl.loop(steps - SLOTS if steps > SLOTS else 0, steps)
    def _(s):
        @pl.loop(0, 8)
        def _(t):
            flush(s, t).wait()

    @pl.loop(0, steps)
    def _(s):
        a_swap(s).wait_send()

    @pl.loop(0, 8)
    def _(t):
        q_forward(t).wait_send()

        @pl.when(jnp.logical_not(jnp.logical_and(at_home, t == c)))
        def _():
            q_push(t).wait_send()


def per_device(steps, matrix, range_basis):
    rows, width = matrix.shape
    depth, basis = range_basis.shape
    w = width // steps // 4
    dma = pltpu.SemaphoreType.DMA
    return pl.pallas_call(
        functools.partial(kernel, steps),
        out_shape=jax.ShapeDtypeStruct((basis, 8 * width), F32),
        in_specs=[pl.BlockSpec(memory_space=pl.ANY)] * 2,
        out_specs=pl.BlockSpec(memory_space=pl.ANY),
        scratch_shapes=[
            pltpu.VMEM((steps, 2 * rows, 2 * w), F32),
            pltpu.VMEM((16 * basis, depth), F32),
            pltpu.VMEM((16 * basis, depth), BF16),
            pltpu.VMEM((16 * basis, depth), BF16),
            pltpu.VMEM((2 * steps, 16 * basis, w), F32),
            pltpu.VMEM((3, 2 * steps, 4 * basis, w), F32),
            pltpu.VMEM((2 * steps, 2 * basis, w), F32),
            pltpu.VMEM((basis, 8 * width), F32),
            dma((steps,)), dma((steps,)), dma((steps,)),
            dma((8,)), dma((8,)), dma((8,)), dma((8,)),
            dma((3, 2, SLOTS)), dma((3, 2, SLOTS)),
            dma((2, SLOTS)), dma((2, SLOTS)), dma((2, SLOTS)), dma((2, SLOTS)),
            dma((SLOTS,)), dma((SLOTS,)), dma((6, SLOTS)), dma((6, SLOTS)), dma((8, SLOTS)),
        ],
        compiler_params=pltpu.CompilerParams(
            collective_id=0, has_side_effects=True, vmem_limit_bytes=60 * 1024 * 1024
        ),
    )(matrix, range_basis.T)


def solution(mesh):
    in_specs = (P("row", "col"), P("col", "row"))
    out_specs = P("row", None)
    return jax.shard_map(
        functools.partial(per_device, STEPS), mesh=mesh, in_specs=in_specs, out_specs=out_specs, check_vma=False
    )
```

time: 367 us -> 177 us (0.48)
  waiting for transfers between devices: 285 us -> 0 us
  Pallas kernels: 0 us -> 166 us
  blocking collectives: 31.8 us -> 0 us
  matrix products: 25.4 us -> 0 us
  between operations: 13.4 us -> 0.01 us
    pallas_call x0 -> x1, Pallas kernels: none -> 166 us  [per_device(): pl.pallas_call(functools.partial(kernel, steps), out_shape=jax.ShapeDtype...]
    all_gather x1 -> x0, waiting for transfers between devices: 148 us -> none  [per_device(): return lax.all_gather(owned_rows, 'col', axis=1, tiled=True)]
    reduce_scatter x1 -> x0, waiting for transfers between devices: 137 us -> none  [per_device(): lax.psum_scatter(project(local_basis, matrix), 'row', scatter_dimension=0...]
    all_to_all x2 -> x0, blocking collectives: 31.8 us -> none  [the longest x1 17 us: copy_for_each(): lax.all_to_all(jnp.broadcast_to(shard[None], (length, *shard.shape)), axi...]
    dot_general x1 -> x0, matrix products: 25.4 us -> none  [project(): lax.dot_general(left, right, (((0,), (0,)), ((), ())), precision=lax.Prec...]
  transfers between devices with their start and end apart: 2 -> 0, of which waited for: 2 -> 0; matrix products, arithmetic and copies ran while one was open for 0% -> 0% of each run, Pallas kernels for 0% -> 0%
where the time goes in v1:
time: 177 us; the launch traced here: 176 us
  Pallas kernels  166 us (94%)
  local copies, waits for them, and re-layouts  10.2 us (6%)
    pallas_call x1, Pallas kernels, per_device(): pl.pallas_call(functools.partial(kernel, steps), out_shape=jax.ShapeDtype...  166 us
    unnamed x1, local copies, waits for them, and re-layouts  10.2 us

profile of v1, /device:TPU:0, one launch (start us, length us, event | category | flops | bytes accessed | tf_op | source)
XLA Modules:
  0.0 176.5 jit_solution(1090609736238253396)
XLA Ops:
  0.0 166.3 %shard_map.28 = f32[24,131072]{1,0:T(8,128)} custom-call(f32[216,16384]{1,0:T(8,128)} %a_ref.1, f32[24,432]{1,0:T(8,128)} %bitcast.1), custom_call_target="tpu_custom_call" | custom-call | tf_op jit(solution)/shard_map/pallas_call | solution.py:320
  166.3 10.2 %copy.4 = f32[24,131072]{1,0:T(8,128)} copy(f32[24,131072]{1,0:T(8,128)} %shard_map.28) | data formatting | bytes 25165824

commit v2 on v0

v2 whole, which is shorter than its diff:
```python
import functools

import jax
import jax.numpy as jnp
from jax import lax
from jax.experimental import pallas as pl
from jax.experimental.pallas import tpu as pltpu
from jax.sharding import PartitionSpec as P

MESH = pl.DeviceIdType.MESH
UNITS = 32
SLOTS = 16
AHEAD = 6
F32 = jnp.float32
BF16 = jnp.bfloat16
Z_LAGS = (-2, 2, 4, 6)
Y_LAG, SPREAD_LAG, FAR_LAG, NEAR_ON_LAG, FAR_ON_LAG, RETIRE_LAG = 7, 8, 9, 10, 12, 14


def halves(value):
    high = value.astype(BF16)
    return high, (value - high.astype(F32)).astype(BF16)


def dot(left, right):
    return jnp.dot(left, right, preferred_element_type=F32)


def kernel(
    units, a_ref, q_ref, out,
    ab, qv, qf, qhi, qlo, p, zr, yr,
    a_own, a_send, a_recv, q_own, q_send, q_recv, f_send, f_recv,
    z_send, z_recv, y_send, y_recv, c_send, c_recv, h_send, h_recv, x_send, x_recv,
):
    rows, width = a_ref.shape
    basis = q_ref.shape[0]
    pair = width // units
    w = pair // 2

    r, c = lax.axis_index("row"), lax.axis_index("col")
    k = lax.rem(r, 2)
    j = lax.div(r, 2)
    z = lax.rem(j, 4)
    ylo = lax.div(j, 4)
    x = lax.rem(c, 4)
    yhi = lax.div(c, 4)

    def row_of(ylo_, z_, k_):
        return (ylo_ * 4 + z_) * 2 + k_

    def wrap(v):
        return lax.rem(v + 8, 4)

    sibling = (row_of(ylo, z, 1 - k), c)
    z_next = [(row_of(ylo, wrap(z + 1), k), c), (row_of(ylo, wrap(z - 1), k), c)]
    y_pair = (row_of(1 - ylo, z, k), c)
    h_pair = [(row_of(1 - ylo, z, k_), (1 - yhi) * 4 + x) for k_ in range(2)]
    x_next = [(r, yhi * 4 + wrap(x + 1)), (r, yhi * 4 + wrap(x - 1))]

    def remote(src, dst, send, recv, device):
        return pltpu.make_async_remote_copy(
            src_ref=src, dst_ref=dst, send_sem=send, recv_sem=recv,
            device_id=device, device_id_type=MESH,
        )

    def slot(u):
        return lax.rem(u, SLOTS)

    def a_local(u):
        cols = pl.ds(pl.multiple_of(u * pair + k * w, 128), w)
        at = pl.ds(pl.multiple_of(k * rows, 8), rows)
        return pltpu.make_async_copy(a_ref.at[:, cols], ab.at[u, at], a_own.at[slot(u)])

    def a_swap(u):
        cols = pl.ds(pl.multiple_of(u * pair + (1 - k) * w, 128), w)
        at = pl.ds(pl.multiple_of(k * rows, 8), rows)
        return remote(a_ref.at[:, cols], ab.at[u, at], a_send.at[slot(u)], a_recv.at[slot(u)], sibling)

    def q_rows(q, k_):
        at = lax.rem(q, 4) * (4 * basis) + lax.div(q, 4) * (2 * basis) + k_ * basis
        return pl.ds(pl.multiple_of(at, 8), basis)

    def q_push(t):
        return remote(qv, qf.at[q_rows(j, k)], q_send.at[t], q_recv.at[j], (c * 2 + k, t))

    def q_here():
        return pltpu.make_async_copy(q_ref, qf.at[q_rows(j, k)], q_recv.at[j])

    def q_landed(q):
        return remote(qv, qf.at[q_rows(q, k)], q_send.at[q], q_recv.at[q], sibling)

    def q_forward(q):
        block = qf.at[q_rows(q, k)]
        return remote(block, block, f_send.at[q], f_recv.at[q], sibling)

    def z_rows(t, d):
        at = wrap(z - (1 - 2 * d) * (t + 1)) * (4 * basis)
        return pl.ds(pl.multiple_of(at, 8), 4 * basis)

    def z_copy(t, d, u):
        return remote(
            p.at[u, z_rows(t, d)], zr.at[t, u], z_send.at[t, slot(u)], z_recv.at[t, slot(u)], z_next[d]
        )

    def y_copy(u):
        return remote(p.at[u, z_rows(3, 0)], yr.at[u], y_send.at[slot(u)], y_recv.at[slot(u)], y_pair)

    def y_rows(ylo_, k_):
        return pl.ds(pl.multiple_of(ylo_ * (2 * basis) + k_ * basis, 8), basis)

    def part_cols(u):
        at = c * width + u * pair + k * w
        return pl.ds(pl.multiple_of(at, 128), w)

    def c_copy(u):
        return remote(
            yr.at[u, y_rows(ylo, 1 - k)], out.at[:, part_cols(u)],
            c_send.at[slot(u)], c_recv.at[slot(u)], sibling,
        )

    def h_copy(k_, u):
        return remote(
            yr.at[u, y_rows(1 - ylo, k_)], out.at[:, part_cols(u)],
            h_send.at[k_, slot(u)], h_recv.at[k, slot(u)], h_pair[k_],
        )

    def h_landed(k_, u):
        return remote(
            yr.at[u, y_rows(1 - ylo, k_)], out.at[:, part_cols(u)],
            h_send.at[k_, slot(u)], h_recv.at[k_, slot(u)], h_pair[k_],
        )

    x_plan = [
        (yhi, x, 0), (yhi, x, 1), (yhi, wrap(x - 1), 0),
        (1 - yhi, x, 0), (1 - yhi, x, 1), (1 - yhi, wrap(x + 1), 1),
    ]

    def x_copy(m, u):
        yhi_, x_, d = x_plan[m]
        at = (yhi_ * 4 + x_) * width + u * pair
        block = out.at[:, pl.ds(pl.multiple_of(at, 128), pair)]
        return remote(block, block, x_send.at[m, slot(u)], x_recv.at[m, slot(u)], x_next[d])

    q_mine = pltpu.make_async_copy(q_ref, qv, q_own)
    q_mine.start()

    @pl.loop(0, AHEAD)
    def _(u):
        a_local(u).start()

    at_home = c == j
    barrier = pltpu.get_barrier_semaphore()
    for device in [sibling, *z_next, y_pair, *h_pair, *x_next]:
        pl.semaphore_signal(barrier, inc=1, device_id=device, device_id_type=MESH)

    @pl.loop(0, 8)
    def _(q):
        @pl.when(jnp.logical_not(jnp.logical_and(at_home, q == j)))
        def _():
            pl.semaphore_signal(barrier, inc=1, device_id=(2 * q + k, j), device_id_type=MESH)

    q_mine.wait()
    pl.semaphore_wait(barrier, 16 - jnp.where(at_home, 1, 0))

    @pl.loop(0, 8)
    def _(t):
        home = jnp.logical_and(at_home, t == c)

        @pl.when(jnp.logical_not(home))
        def _():
            q_push(t).start()

        @pl.when(home)
        def _():
            q_here().start()

    @pl.loop(0, 4)
    def _(u):
        a_swap(u).start()

    @pl.loop(0, 8)
    def _(q):
        q_landed(q).wait_recv()
        q_forward(q).start()

    @pl.loop(4, AHEAD)
    def _(u):
        a_swap(u).start()

    @pl.loop(0, 8)
    def _(q):
        q_forward(q).wait_recv()

    high, low = halves(qf[...])
    qhi[...] = high
    qlo[...] = low

    def compute(d, u):
        a_local(u).wait()
        a_swap(u).wait_recv()
        a_high, a_low = halves(ab[u])
        p[u] = dot(qhi[...], a_low) + dot(qlo[...], a_high) + dot(qhi[...], a_high)
        z_copy(0, d, u).start()

    def fetch(d, u):
        @pl.when(u >= SLOTS)
        def _():
            a_swap(u - SLOTS).wait_send()

        a_local(u).start()
        a_swap(u).start()

    def z_step(t):
        def body(d, u):
            z_copy(t - 1, d, u).wait_recv()
            at = z_rows(t, d)
            p[u, at] = p[u, at] + zr[t - 1, u]
            if t < 3:
                z_copy(t, d, u).start()
            else:
                y_copy(u).start()
        return body

    def y_last(d, u):
        y_copy(u).wait_recv()
        total = p[u, z_rows(3, 0)] + yr[u]
        yr[u] = total
        c_copy(u).start()
        for k_ in range(2):
            h_copy(k_, u).start()
        out[:, part_cols(u)] = yr[u, y_rows(ylo, k)]

    def spread(d, u):
        c_copy(u).wait_recv()
        x_copy(0, u).start()
        x_copy(1, u).start()

    def spread_far(d, u):
        for k_ in range(2):
            h_landed(k_, u).wait_recv()
        x_copy(3, u).start()
        x_copy(4, u).start()

    def forward(m, first):
        def body(d, u):
            x_copy(first, u).wait_recv()
            x_copy(m, u).start()
        return body

    def retire(d, u):
        for t in range(3):
            z_copy(t, d, u).wait_send()
        y_copy(u).wait_send()
        c_copy(u).wait_send()
        for k_ in range(2):
            h_copy(k_, u).wait_send()
        for m in (1, 2, 3, 5):
            x_copy(m, u).wait_recv()
        for m in range(6):
            x_copy(m, u).wait_send()

    for d in range(2):
        compute(d, d)

    @pl.loop(0, (units + RETIRE_LAG) // 2)
    def _(i):
        for d in range(2):
            def live(lag, body):
                u = 2 * i + d - lag

                @pl.when(jnp.logical_and(u >= max(-lag, 0), u < units))
                def _():
                    body((d - lag) % 2, u)

            live(RETIRE_LAG, retire)
            live(-AHEAD, fetch)
            for t in (3, 2, 1):
                live(Z_LAGS[t], z_step(t))
            live(Z_LAGS[0], compute)
            live(SPREAD_LAG, spread)
            live(FAR_LAG, spread_far)
            live(NEAR_ON_LAG, forward(2, 0))
            live(FAR_ON_LAG, forward(5, 4))
            live(Y_LAG, y_last)

    @pl.loop(units - SLOTS, units)
    def _(u):
        a_swap(u).wait_send()

    @pl.loop(0, 8)
    def _(t):
        q_forward(t).wait_send()

        @pl.when(jnp.logical_not(jnp.logical_and(at_home, t == c)))
        def _():
            q_push(t).wait_send()


def per_device(units, matrix, range_basis):
    rows, width = matrix.shape
    depth, basis = range_basis.shape
    w = width // units // 2
    dma = pltpu.SemaphoreType.DMA
    ring = dma((SLOTS,))
    return pl.pallas_call(
        functools.partial(kernel, units),
        out_shape=pltpu.VMEM((basis, 8 * width), F32),
        in_specs=[pl.BlockSpec(memory_space=pl.ANY)] * 2,
        out_specs=pl.BlockSpec(memory_space=pltpu.VMEM),
        scratch_shapes=[
            pltpu.VMEM((units, 2 * rows, w), F32),
            pltpu.VMEM((basis, depth), F32),
            pltpu.VMEM((16 * basis, depth), F32),
            pltpu.VMEM((16 * basis, depth), BF16),
            pltpu.VMEM((16 * basis, depth), BF16),
            pltpu.VMEM((units, 16 * basis, w), F32),
            pltpu.VMEM((3, units, 4 * basis, w), F32),
            pltpu.VMEM((units, 4 * basis, w), F32),
            ring, ring, ring,
            dma, dma((8,)), dma((8,)), dma((8,)), dma((8,)),
            dma((3, SLOTS)), dma((3, SLOTS)), ring, ring, ring, ring,
            dma((2, SLOTS)), dma((2, SLOTS)), dma((6, SLOTS)), dma((6, SLOTS)),
        ],
        compiler_params=pltpu.CompilerParams(
            collective_id=0, has_side_effects=True, vmem_limit_bytes=46 * 1024 * 1024
        ),
    )(matrix, range_basis.T)


def solution(mesh):
    in_specs = (P("row", "col"), P("col", "row"))
    out_specs = P("row", None)
    return jax.shard_map(
        functools.partial(per_device, UNITS), mesh=mesh, in_specs=in_specs, out_specs=out_specs, check_vma=False
    )
```

time: 367 us -> 163 us (0.44)
  waiting for transfers between devices: 285 us -> 0 us
  Pallas kernels: 0 us -> 157 us
  blocking collectives: 31.8 us -> 0 us
  matrix products: 25.4 us -> 0 us
  between operations: 13.4 us -> 0.01 us
  local copies, waits for them, and re-layouts: 11.6 us -> 4.78 us
    pallas_call x0 -> x1, Pallas kernels: none -> 157 us  [per_device(): pl.pallas_call(functools.partial(kernel, units), out_shape=pltpu.VMEM((ba...]
    all_gather x1 -> x0, waiting for transfers between devices: 148 us -> none  [per_device(): return lax.all_gather(owned_rows, 'col', axis=1, tiled=True)]
    reduce_scatter x1 -> x0, waiting for transfers between devices: 137 us -> none  [per_device(): lax.psum_scatter(project(local_basis, matrix), 'row', scatter_dimension=0...]
    all_to_all x2 -> x0, blocking collectives: 31.8 us -> none  [the longest x1 17 us: copy_for_each(): lax.all_to_all(jnp.broadcast_to(shard[None], (length, *shard.shape)), axi...]
    dot_general x1 -> x0, matrix products: 25.4 us -> none  [project(): lax.dot_general(left, right, (((0,), (0,)), ((), ())), precision=lax.Prec...]
    unnamed x1, local copies, waits for them, and re-layouts: 10.2 us -> 4.78 us
  transfers between devices with their start and end apart: 2 -> 0, of which waited for: 2 -> 0; matrix products, arithmetic and copies ran while one was open for 0% -> 0% of each run, Pallas kernels for 0% -> 0%
where the time goes in v2:
time: 163 us; the launch traced here: 162 us
  Pallas kernels  157 us (96%)
  local copies, waits for them, and re-layouts  4.78 us (3%)
    pallas_call x1, Pallas kernels, per_device(): pl.pallas_call(functools.partial(kernel, units), out_shape=pltpu.VMEM((ba...  157 us
    unnamed x1, local copies, waits for them, and re-layouts  4.78 us

profile of v2, /device:TPU:0, one launch (start us, length us, event | category | flops | bytes accessed | tf_op | source)
XLA Modules:
  0.0 161.7 jit_solution(18441686692182310659)
XLA Ops:
  0.0 156.9 %shard_map.28 = f32[24,131072]{1,0:T(8,128)S(1)} custom-call(f32[216,16384]{1,0:T(8,128)} %a_ref.1, f32[24,432]{1,0:T(8,128)} %bitcast.1), custom_call_target="tpu_custom_call" | custom-call | tf_op jit(solution)/shard_map/pallas_call | solution.py:305
  156.9 4.8 %copy.4 = f32[24,131072]{1,0:T(8,128)} copy(f32[24,131072]{1,0:T(8,128)S(1)} %shard_map.28) | data formatting | bytes 25165824

commit v3 on v2

--- a/solution.py
+++ b/solution.py
@@ -8,13 +8,25 @@
 from jax.sharding import PartitionSpec as P
 
 MESH = pl.DeviceIdType.MESH
-UNITS = 32
-SLOTS = 16
+UNITS = 64
+SHORT, LONG = 8, 16
 AHEAD = 6
 F32 = jnp.float32
 BF16 = jnp.bfloat16
-Z_LAGS = (-2, 2, 4, 6)
-Y_LAG, SPREAD_LAG, FAR_LAG, NEAR_ON_LAG, FAR_ON_LAG, RETIRE_LAG = 7, 8, 9, 10, 12, 14
+STAGES = (
+    ("z1", 0),
+    ("far_on", 12),
+    ("compute", -3),
+    ("z0", -3),
+    ("z3", 5),
+    ("spread", 8),
+    ("retire", 14),
+    ("fetch", -AHEAD),
+    ("y", 7),
+    ("far", 9),
+    ("z2", 2),
+    ("near_on", 10),
+)
 
 
 def halves(value):
@@ -30,7 +42,7 @@
     units, a_ref, q_ref, out,
     ab, qv, qf, qhi, qlo, p, zr, yr,
     a_own, a_send, a_recv, q_own, q_send, q_recv, f_send, f_recv,
-    z_send, z_recv, y_send, y_recv, c_send, c_recv, h_send, h_recv, x_send, x_recv,
+    sent, z_recv, y_recv, c_recv, h_recv, x_recv, x_rest,
 ):
     rows, width = a_ref.shape
     basis = q_ref.shape[0]
@@ -63,35 +75,42 @@
             device_id=device, device_id_type=MESH,
         )
 
-    def slot(u):
-        return lax.rem(u, SLOTS)
+    def short(u):
+        return lax.rem(u, SHORT)
+
+    def long(u):
+        return lax.rem(u, LONG)
 
     def a_local(u):
         cols = pl.ds(pl.multiple_of(u * pair + k * w, 128), w)
         at = pl.ds(pl.multiple_of(k * rows, 8), rows)
-        return pltpu.make_async_copy(a_ref.at[:, cols], ab.at[u, at], a_own.at[slot(u)])
+        return pltpu.make_async_copy(a_ref.at[:, cols], ab.at[u, at], a_own.at[short(u)])
 
     def a_swap(u):
         cols = pl.ds(pl.multiple_of(u * pair + (1 - k) * w, 128), w)
         at = pl.ds(pl.multiple_of(k * rows, 8), rows)
-        return remote(a_ref.at[:, cols], ab.at[u, at], a_send.at[slot(u)], a_recv.at[slot(u)], sibling)
+        return remote(a_ref.at[:, cols], ab.at[u, at], a_send.at[long(u)], a_recv.at[long(u)], sibling)
 
     def q_rows(q, k_):
         at = lax.rem(q, 4) * (4 * basis) + lax.div(q, 4) * (2 * basis) + k_ * basis
         return pl.ds(pl.multiple_of(at, 8), basis)
 
     def q_push(t):
-        return remote(qv, qf.at[q_rows(j, k)], q_send.at[t], q_recv.at[j], (c * 2 + k, t))
+        return remote(qv, qf.at[q_rows(j, k)], q_send, q_recv.at[j], (c * 2 + k, t))
 
     def q_here():
         return pltpu.make_async_copy(q_ref, qf.at[q_rows(j, k)], q_recv.at[j])
 
     def q_landed(q):
-        return remote(qv, qf.at[q_rows(q, k)], q_send.at[q], q_recv.at[q], sibling)
+        return remote(qv, qf.at[q_rows(q, k)], q_send, q_recv.at[q], sibling)
 
     def q_forward(q):
         block = qf.at[q_rows(q, k)]
-        return remote(block, block, f_send.at[q], f_recv.at[q], sibling)
+        return remote(block, block, f_send, f_recv, sibling)
+
+    def q_amount(blocks, sem):
+        part = qf.at[pl.ds(0, blocks * basis)]
+        return pltpu.make_async_copy(part, part, sem)
 
     def z_rows(t, d):
         at = wrap(z - (1 - 2 * d) * (t + 1)) * (4 * basis)
@@ -99,11 +118,11 @@
 
     def z_copy(t, d, u):
         return remote(
-            p.at[u, z_rows(t, d)], zr.at[t, u], z_send.at[t, slot(u)], z_recv.at[t, slot(u)], z_next[d]
+            p.at[u, z_rows(t, d)], zr.at[t, u], sent.at[long(u)], z_recv.at[t, short(u)], z_next[d]
         )
 
     def y_copy(u):
-        return remote(p.at[u, z_rows(3, 0)], yr.at[u], y_send.at[slot(u)], y_recv.at[slot(u)], y_pair)
+        return remote(p.at[u, z_rows(3, 0)], yr.at[u], sent.at[long(u)], y_recv.at[short(u)], y_pair)
 
     def y_rows(ylo_, k_):
         return pl.ds(pl.multiple_of(ylo_ * (2 * basis) + k_ * basis, 8), basis)
@@ -115,20 +134,22 @@
     def c_copy(u):
         return remote(
             yr.at[u, y_rows(ylo, 1 - k)], out.at[:, part_cols(u)],
-            c_send.at[slot(u)], c_recv.at[slot(u)], sibling,
+            sent.at[long(u)], c_recv.at[short(u)], sibling,
         )
 
     def h_copy(k_, u):
         return remote(
             yr.at[u, y_rows(1 - ylo, k_)], out.at[:, part_cols(u)],
-            h_send.at[k_, slot(u)], h_recv.at[k, slot(u)], h_pair[k_],
+            sent.at[long(u)], h_recv.at[short(u)], h_pair[k_],
         )
 
-    def h_landed(k_, u):
-        return remote(
-            yr.at[u, y_rows(1 - ylo, k_)], out.at[:, part_cols(u)],
-            h_send.at[k_, slot(u)], h_recv.at[k_, slot(u)], h_pair[k_],
-        )
+    def block_of(yhi_, x_, u):
+        at = (yhi_ * 4 + x_) * width + u * pair
+        return out.at[:, pl.ds(pl.multiple_of(at, 128), pair)]
+
+    def h_landed(u):
+        block = block_of(1 - yhi, x, u)
+        return remote(block, block, sent.at[long(u)], h_recv.at[short(u)], sibling)
 
     x_plan = [
         (yhi, x, 0), (yhi, x, 1), (yhi, wrap(x - 1), 0),
@@ -137,9 +158,18 @@
 
     def x_copy(m, u):
         yhi_, x_, d = x_plan[m]
-        at = (yhi_ * 4 + x_) * width + u * pair
-        block = out.at[:, pl.ds(pl.multiple_of(at, 128), pair)]
-        return remote(block, block, x_send.at[m, slot(u)], x_recv.at[m, slot(u)], x_next[d])
+        block = block_of(yhi_, x_, u)
+        recv = {0: x_recv.at[0, short(u)], 4: x_recv.at[1, short(u)]}.get(m, x_rest.at[long(u)])
+        return remote(block, block, sent.at[long(u)], recv, x_next[d])
+
+    def amount(strips):
+        return out.at[:, pl.ds(0, strips * w)]
+
+    def retired(u):
+        return pltpu.make_async_copy(amount(31), amount(31), sent.at[long(u)])
+
+    def rest_landed(u):
+        return pltpu.make_async_copy(amount(8), amount(8), x_rest.at[long(u)])
 
     q_mine = pltpu.make_async_copy(q_ref, qv, q_own)
     q_mine.start()
@@ -187,10 +217,7 @@
     def _(u):
         a_swap(u).start()
 
-    @pl.loop(0, 8)
-    def _(q):
-        q_forward(q).wait_recv()
-
+    q_amount(8, f_recv).wait()
     high, low = halves(qf[...])
     qhi[...] = high
     qlo[...] = low
@@ -200,12 +227,14 @@
         a_swap(u).wait_recv()
         a_high, a_low = halves(ab[u])
         p[u] = dot(qhi[...], a_low) + dot(qlo[...], a_high) + dot(qhi[...], a_high)
+
+    def z_first(d, u):
         z_copy(0, d, u).start()
 
     def fetch(d, u):
-        @pl.when(u >= SLOTS)
+        @pl.when(u >= LONG)
         def _():
-            a_swap(u - SLOTS).wait_send()
+            a_swap(u - LONG).wait_send()
 
         a_local(u).start()
         a_swap(u).start()
@@ -236,8 +265,7 @@
         x_copy(1, u).start()
 
     def spread_far(d, u):
-        for k_ in range(2):
-            h_landed(k_, u).wait_recv()
+        h_landed(u).wait_recv()
         x_copy(3, u).start()
         x_copy(4, u).start()
 
@@ -248,52 +276,43 @@
         return body
 
     def retire(d, u):
-        for t in range(3):
-            z_copy(t, d, u).wait_send()
-        y_copy(u).wait_send()
-        c_copy(u).wait_send()
-        for k_ in range(2):
-            h_copy(k_, u).wait_send()
-        for m in (1, 2, 3, 5):
-            x_copy(m, u).wait_recv()
-        for m in range(6):
-            x_copy(m, u).wait_send()
-
-    for d in range(2):
-        compute(d, d)
-
-    @pl.loop(0, (units + RETIRE_LAG) // 2)
+        rest_landed(u).wait()
+        retired(u).wait()
+
+    bodies = {
+        "retire": retire, "fetch": fetch, "z3": z_step(3), "z2": z_step(2), "z1": z_step(1), "z0": z_first,
+        "compute": compute, "y": y_last, "spread": spread, "far": spread_far,
+        "near_on": forward(2, 0), "far_on": forward(5, 4),
+    }
+    lags = dict(STAGES)
+    for u in range(-min(lags["compute"], lags["z0"])):
+        for name in ("compute", "z0"):
+            if u < -lags[name]:
+                bodies[name](u % 2, u)
+
+    @pl.loop(0, (units + max(lags.values()) + 1) // 2)
     def _(i):
         for d in range(2):
-            def live(lag, body):
+            for name, lag in STAGES:
                 u = 2 * i + d - lag
 
                 @pl.when(jnp.logical_and(u >= max(-lag, 0), u < units))
                 def _():
-                    body((d - lag) % 2, u)
-
-            live(RETIRE_LAG, retire)
-            live(-AHEAD, fetch)
-            for t in (3, 2, 1):
-                live(Z_LAGS[t], z_step(t))
-            live(Z_LAGS[0], compute)
-            live(SPREAD_LAG, spread)
-            live(FAR_LAG, spread_far)
-            live(NEAR_ON_LAG, forward(2, 0))
-            live(FAR_ON_LAG, forward(5, 4))
-            live(Y_LAG, y_last)
-
-    @pl.loop(units - SLOTS, units)
+                    bodies[name]((d - lag) % 2, u)
+
+    @pl.loop(units - LONG, units)
     def _(u):
         a_swap(u).wait_send()
 
-    @pl.loop(0, 8)
-    def _(t):
-        q_forward(t).wait_send()
-
-        @pl.when(jnp.logical_not(jnp.logical_and(at_home, t == c)))
-        def _():
-            q_push(t).wait_send()
+    q_amount(8, f_send).wait()
+
+    @pl.when(at_home)
+    def _():
+        q_amount(7, q_send).wait()
+
+    @pl.when(jnp.logical_not(at_home))
+    def _():
+        q_amount(8, q_send).wait()
 
 
 def per_device(units, matrix, range_basis):
@@ -301,7 +320,7 @@
     depth, basis = range_basis.shape
     w = width // units // 2
     dma = pltpu.SemaphoreType.DMA
-    ring = dma((SLOTS,))
+    short, long = dma((SHORT,)), dma((LONG,))
     return pl.pallas_call(
         functools.partial(kernel, units),
         out_shape=pltpu.VMEM((basis, 8 * width), F32),
@@ -316,10 +335,8 @@
             pltpu.VMEM((units, 16 * basis, w), F32),
             pltpu.VMEM((3, units, 4 * basis, w), F32),
             pltpu.VMEM((units, 4 * basis, w), F32),
-            ring, ring, ring,
-            dma, dma((8,)), dma((8,)), dma((8,)), dma((8,)),
-            dma((3, SLOTS)), dma((3, SLOTS)), ring, ring, ring, ring,
-            dma((2, SLOTS)), dma((2, SLOTS)), dma((6, SLOTS)), dma((6, SLOTS)),
+            short, long, long, dma, dma, dma((8,)), dma, dma,
+            long, dma((3, SHORT)), short, short, short, dma((2, SHORT)), long,
         ],
         compiler_params=pltpu.CompilerParams(
             collective_id=0, has_side_effects=True, vmem_limit_bytes=46 * 1024 * 1024

time: 163 us -> 150 us (0.920)
  Pallas kernels: 157 us -> 145 us
    pallas_call x1, Pallas kernels: 157 us -> 145 us  [per_device(): pl.pallas_call(functools.partial(kernel, units), out_shape=pltpu.VMEM((ba...]
where the time goes in v3:
time: 150 us
  Pallas kernels  145 us (97%)
  local copies, waits for them, and re-layouts  4.78 us (3%)
    pallas_call x1, Pallas kernels, per_device(): pl.pallas_call(functools.partial(kernel, units), out_shape=pltpu.VMEM((ba...  145 us
    unnamed x1, local copies, waits for them, and re-layouts  4.78 us

profile of v3, /device:TPU:0, one launch (start us, length us, event | category | flops | bytes accessed | tf_op | source)
XLA Modules:
  0.0 150.0 jit_solution(18429528860347875328)
XLA Ops:
  0.0 145.2 %shard_map.28 = f32[24,131072]{1,0:T(8,128)S(1)} custom-call(f32[216,16384]{1,0:T(8,128)} %a_ref.1, f32[24,432]{1,0:T(8,128)} %bitcast.1), custom_call_target="tpu_custom_call" | custom-call | tf_op jit(solution)/shard_map/pallas_call | solution.py:324
  145.2 4.8 %copy.4 = f32[24,131072]{1,0:T(8,128)} copy(f32[24,131072]{1,0:T(8,128)S(1)} %shard_map.28) | data formatting | bytes 25165824

commit v4 on v3

--- a/solution.py
+++ b/solution.py
@@ -9,23 +9,13 @@
 
 MESH = pl.DeviceIdType.MESH
 UNITS = 64
-SHORT, LONG = 8, 16
+SHORT, LONG = 10, 16
 AHEAD = 6
 F32 = jnp.float32
 BF16 = jnp.bfloat16
 STAGES = (
-    ("z1", 0),
-    ("far_on", 12),
-    ("compute", -3),
-    ("z0", -3),
-    ("z3", 5),
-    ("spread", 8),
-    ("retire", 14),
-    ("fetch", -AHEAD),
-    ("y", 7),
-    ("far", 9),
-    ("z2", 2),
-    ("near_on", 10),
+    ("spread", 7), ("far_on", 11), ("z1", 1), ("y", 6), ("compute", -2), ("z0", -2), ("far", 8), ("near_on", 9),
+    ("z2", 3), ("retire", 13), ("fetch", -AHEAD),
 )
 
 
@@ -112,17 +102,18 @@
         part = qf.at[pl.ds(0, blocks * basis)]
         return pltpu.make_async_copy(part, part, sem)
 
-    def z_rows(t, d):
-        at = wrap(z - (1 - 2 * d) * (t + 1)) * (4 * basis)
-        return pl.ds(pl.multiple_of(at, 8), 4 * basis)
-
-    def z_copy(t, d, u):
+    def z_rows(away):
+        return pl.ds(pl.multiple_of(wrap(z + away) * (4 * basis), 8), 4 * basis)
+
+    def z_copy(kind, d, u):
+        ahead = 1 - 2 * d
+        away, way = ((2 * ahead, d), (ahead, d), (-ahead, 1 - d))[kind]
         return remote(
-            p.at[u, z_rows(t, d)], zr.at[t, u], sent.at[long(u)], z_recv.at[t, short(u)], z_next[d]
+            p.at[u, z_rows(away)], zr.at[kind, u], sent.at[long(u)], z_recv.at[kind, short(u)], z_next[way]
         )
 
     def y_copy(u):
-        return remote(p.at[u, z_rows(3, 0)], yr.at[u], sent.at[long(u)], y_recv.at[short(u)], y_pair)
+        return remote(p.at[u, z_rows(0)], yr.at[u], sent.at[long(u)], y_recv.at[short(u)], y_pair)
 
     def y_rows(ylo_, k_):
         return pl.ds(pl.multiple_of(ylo_ * (2 * basis) + k_ * basis, 8), basis)
@@ -193,7 +184,8 @@
     pl.semaphore_wait(barrier, 16 - jnp.where(at_home, 1, 0))
 
     @pl.loop(0, 8)
-    def _(t):
+    def _(n):
+        t = lax.rem(yhi + lax.rem(n, 2), 2) * 4 + lax.rem(x + 6 - lax.div(n, 2), 4)
         home = jnp.logical_and(at_home, t == c)
 
         @pl.when(jnp.logical_not(home))
@@ -229,6 +221,7 @@
         p[u] = dot(qhi[...], a_low) + dot(qlo[...], a_high) + dot(qhi[...], a_high)
 
     def z_first(d, u):
+        z_copy(2, d, u).start()
         z_copy(0, d, u).start()
 
     def fetch(d, u):
@@ -239,20 +232,22 @@
         a_local(u).start()
         a_swap(u).start()
 
-    def z_step(t):
-        def body(d, u):
-            z_copy(t - 1, d, u).wait_recv()
-            at = z_rows(t, d)
-            p[u, at] = p[u, at] + zr[t - 1, u]
-            if t < 3:
-                z_copy(t, d, u).start()
-            else:
-                y_copy(u).start()
-        return body
+    def z_on(d, u):
+        z_copy(0, d, u).wait_recv()
+        at = z_rows(1 - 2 * d)
+        p[u, at] = p[u, at] + zr[0, u]
+        z_copy(1, d, u).start()
+
+    def z_last(d, u):
+        z_copy(1, d, u).wait_recv()
+        z_copy(2, d, u).wait_recv()
+        at = z_rows(0)
+        p[u, at] = p[u, at] + (zr[1, u] + zr[2, u])
+        y_copy(u).start()
 
     def y_last(d, u):
         y_copy(u).wait_recv()
-        total = p[u, z_rows(3, 0)] + yr[u]
+        total = p[u, z_rows(0)] + yr[u]
         yr[u] = total
         c_copy(u).start()
         for k_ in range(2):
@@ -280,7 +275,7 @@
         retired(u).wait()
 
     bodies = {
-        "retire": retire, "fetch": fetch, "z3": z_step(3), "z2": z_step(2), "z1": z_step(1), "z0": z_first,
+        "retire": retire, "fetch": fetch, "z2": z_last, "z1": z_on, "z0": z_first,
         "compute": compute, "y": y_last, "spread": spread, "far": spread_far,
         "near_on": forward(2, 0), "far_on": forward(5, 4),
     }

time: 150 us -> 147 us (0.980)
  Pallas kernels: 145 us -> 142 us
    pallas_call x1, Pallas kernels: 145 us -> 142 us  [per_device(): pl.pallas_call(functools.partial(kernel, units), out_shape=pltpu.VMEM((ba...]
where the time goes in v4:
time: 147 us
  Pallas kernels  142 us (97%)
  local copies, waits for them, and re-layouts  4.78 us (3%)
    pallas_call x1, Pallas kernels, per_device(): pl.pallas_call(functools.partial(kernel, units), out_shape=pltpu.VMEM((ba...  142 us
    unnamed x1, local copies, waits for them, and re-layouts  4.78 us

profile of v4, /device:TPU:0, one launch (start us, length us, event | category | flops | bytes accessed | tf_op | source)
XLA Modules:
  0.0 146.7 jit_solution(5946747460723172007)
XLA Ops:
  0.0 141.9 %shard_map.28 = f32[24,131072]{1,0:T(8,128)S(1)} custom-call(f32[216,16384]{1,0:T(8,128)} %a_ref.1, f32[24,432]{1,0:T(8,128)} %bitcast.1), custom_call_target="tpu_custom_call" | custom-call | tf_op jit(solution)/shard_map/pallas_call | solution.py:319
  141.9 4.8 %copy.4 = f32[24,131072]{1,0:T(8,128)} copy(f32[24,131072]{1,0:T(8,128)S(1)} %shard_map.28) | data formatting | bytes 25165824

commit v5 on v4

--- a/solution.py
+++ b/solution.py
@@ -79,7 +79,7 @@
     def a_swap(u):
         cols = pl.ds(pl.multiple_of(u * pair + (1 - k) * w, 128), w)
         at = pl.ds(pl.multiple_of(k * rows, 8), rows)
-        return remote(a_ref.at[:, cols], ab.at[u, at], a_send.at[long(u)], a_recv.at[long(u)], sibling)
+        return remote(a_ref.at[:, cols], ab.at[u, at], a_send, a_recv.at[long(u)], sibling)
 
     def q_rows(q, k_):
         at = lax.rem(q, 4) * (4 * basis) + lax.div(q, 4) * (2 * basis) + k_ * basis
@@ -162,30 +162,30 @@
     def rest_landed(u):
         return pltpu.make_async_copy(amount(8), amount(8), x_rest.at[long(u)])
 
-    q_mine = pltpu.make_async_copy(q_ref, qv, q_own)
-    q_mine.start()
-
-    @pl.loop(0, AHEAD)
-    def _(u):
-        a_local(u).start()
-
     at_home = c == j
     barrier = pltpu.get_barrier_semaphore()
-    for device in [sibling, *z_next, y_pair, *h_pair, *x_next]:
-        pl.semaphore_signal(barrier, inc=1, device_id=device, device_id_type=MESH)
-
     @pl.loop(0, 8)
     def _(q):
         @pl.when(jnp.logical_not(jnp.logical_and(at_home, q == j)))
         def _():
             pl.semaphore_signal(barrier, inc=1, device_id=(2 * q + k, j), device_id_type=MESH)
 
+    for device in [sibling, *z_next, y_pair, *h_pair, *x_next]:
+        pl.semaphore_signal(barrier, inc=1, device_id=device, device_id_type=MESH)
+
+    q_mine = pltpu.make_async_copy(q_ref, qv, q_own)
+    q_mine.start()
+
+    @pl.loop(0, AHEAD)
+    def _(u):
+        a_local(u).start()
+
     q_mine.wait()
     pl.semaphore_wait(barrier, 16 - jnp.where(at_home, 1, 0))
 
     @pl.loop(0, 8)
     def _(n):
-        t = lax.rem(yhi + lax.rem(n, 2), 2) * 4 + lax.rem(x + 6 - lax.div(n, 2), 4)
+        t = lax.rem(yhi + 1 + lax.div(n, 4), 2) * 4 + lax.rem(x + 6 - lax.rem(n, 4), 4)
         home = jnp.logical_and(at_home, t == c)
 
         @pl.when(jnp.logical_not(home))
@@ -225,10 +225,6 @@
         z_copy(0, d, u).start()
 
     def fetch(d, u):
-        @pl.when(u >= LONG)
-        def _():
-            a_swap(u - LONG).wait_send()
-
         a_local(u).start()
         a_swap(u).start()
 
@@ -295,9 +291,8 @@
                 def _():
                     bodies[name]((d - lag) % 2, u)
 
-    @pl.loop(units - LONG, units)
-    def _(u):
-        a_swap(u).wait_send()
+    swapped = ab.at[pl.ds(0, units // 2)]
+    pltpu.make_async_copy(swapped, swapped, a_send).wait()
 
     q_amount(8, f_send).wait()
 
@@ -330,7 +325,7 @@
             pltpu.VMEM((units, 16 * basis, w), F32),
             pltpu.VMEM((3, units, 4 * basis, w), F32),
             pltpu.VMEM((units, 4 * basis, w), F32),
-            short, long, long, dma, dma, dma((8,)), dma, dma,
+            short, dma, long, dma, dma, dma((8,)), dma, dma,
             long, dma((3, SHORT)), short, short, short, dma((2, SHORT)), long,
         ],
         compiler_params=pltpu.CompilerParams(

time: 147 us -> 147 us (level)
  no operation moved by 1% of the time
where the time goes in v5:
time: 147 us; the launch traced here: 146 us
  Pallas kernels  142 us (97%)
  local copies, waits for them, and re-layouts  4.78 us (3%)
    pallas_call x1, Pallas kernels, per_device(): pl.pallas_call(functools.partial(kernel, units), out_shape=pltpu.VMEM((ba...  142 us
    unnamed x1, local copies, waits for them, and re-layouts  4.78 us

profile of v5, /device:TPU:0, one launch (start us, length us, event | category | flops | bytes accessed | tf_op | source)
XLA Modules:
  0.0 146.5 jit_solution(3431139901223865227)
XLA Ops:
  0.0 141.7 %shard_map.28 = f32[24,131072]{1,0:T(8,128)S(1)} custom-call(f32[216,16384]{1,0:T(8,128)} %a_ref.1, f32[24,432]{1,0:T(8,128)} %bitcast.1), custom_call_target="tpu_custom_call" | custom-call | tf_op jit(solution)/shard_map/pallas_call | solution.py:314
  141.7 4.8 %copy.4 = f32[24,131072]{1,0:T(8,128)} copy(f32[24,131072]{1,0:T(8,128)S(1)} %shard_map.28) | data formatting | bytes 25165824

commit v6 on v5

--- a/solution.py
+++ b/solution.py
@@ -14,8 +14,17 @@
 F32 = jnp.float32
 BF16 = jnp.bfloat16
 STAGES = (
-    ("spread", 7), ("far_on", 11), ("z1", 1), ("y", 6), ("compute", -2), ("z0", -2), ("far", 8), ("near_on", 9),
-    ("z2", 3), ("retire", 13), ("fetch", -AHEAD),
+    ("z1", 1),
+    ("spread", 7),
+    ("compute", -2),
+    ("z0", -2),
+    ("far_on", 11),
+    ("y", 6),
+    ("far", 8),
+    ("near_on", 9),
+    ("z2", 3),
+    ("retire", 13),
+    ("fetch", -AHEAD),
 )
 
 

time: 147 us -> 147 us (level)
  no operation moved by 1% of the time
where the time goes in v6:
time: 147 us; the launch traced here: 145 us
  Pallas kernels  141 us (96%)
  local copies, waits for them, and re-layouts  4.78 us (3%)
    pallas_call x1, Pallas kernels, per_device(): pl.pallas_call(functools.partial(kernel, units), out_shape=pltpu.VMEM((ba...  141 us
    unnamed x1, local copies, waits for them, and re-layouts  4.78 us

profile of v6, /device:TPU:0, one launch (start us, length us, event | category | flops | bytes accessed | tf_op | source)
XLA Modules:
  0.0 145.3 jit_solution(8076197568089919251)
XLA Ops:
  0.0 140.5 %shard_map.28 = f32[24,131072]{1,0:T(8,128)S(1)} custom-call(f32[216,16384]{1,0:T(8,128)} %a_ref.1, f32[24,432]{1,0:T(8,128)} %bitcast.1), custom_call_target="tpu_custom_call" | custom-call | tf_op jit(solution)/shard_map/pallas_call | solution.py:323
  140.6 4.8 %copy.4 = f32[24,131072]{1,0:T(8,128)} copy(f32[24,131072]{1,0:T(8,128)S(1)} %shard_map.28) | data formatting | bytes 25165824
